TPU v7x, 32 devices: a whole 2x2x4 slice. The times are simulated.
32 devices in a mesh: dp: 16 (over z, x, core), mp: 2 (over y).
Axes of the slice: x: 2, y: 2, z: 4, core: 2. Of those that a mesh axis runs over, the one named last changes fastest.
Arguments:
- inputs: bfloat16 [8192, 2048], P(('dp', 'mp')), may hold values from -6 to 6
- segment_ids: int32 [16, 512], P('dp'), may hold values from 0 to 3, never falling along the last dimension, each value on 1 to 256 neighbouring positions
- norm1_gain: float32 [2048], replicated, may hold values from 0.5 to 1.5
- norm1_shift: float32 [2048], replicated, may hold values from -3 to 3
- qkv_weight: bfloat16 [3, 2048, 2048], P(None, 'dp', 'mp'), may hold values from -0.125 to 0.125
- qkv_bias: float32 [3, 2048], P(None, 'mp'), may hold values from -64 to 64
- out_weight: bfloat16 [2048, 2048], P('mp', 'dp'), may hold values from -0.5 to 0.5
- norm2_gain: float32 [2048], replicated, may hold values from 0.5 to 1.5
- norm2_shift: float32 [2048], replicated, may hold values from -3 to 3
- gate_weight: bfloat16 [2048, 5632], P('dp', 'mp'), may hold values from -0.125 to 0.125
- up_weight: bfloat16 [2048, 5632], P('dp', 'mp'), may hold values from -0.125 to 0.125
- down_weight: bfloat16 [5632, 2048], P('mp', 'dp'), may hold values from -0.078125 to 0.078125
- cotangent: bfloat16 [8192, 2048], P(('dp', 'mp')), may hold values from -6 to 6
Outputs:
- output: bfloat16 [8192, 2048], P(('dp', 'mp'))
- input_grad: float32 [8192, 2048], P(('dp', 'mp'))
- norm1_gain_grad: float32 [2048], replicated
- norm1_shift_grad: float32 [2048], replicated
- qkv_weight_grad: float32 [3, 2048, 2048], P(None, 'dp', 'mp')
- qkv_bias_grad: float32 [3, 2048], P(None, 'mp')
- out_weight_grad: float32 [2048, 2048], P('mp', 'dp')
- norm2_gain_grad: float32 [2048], replicated
- norm2_shift_grad: float32 [2048], replicated
- gate_weight_grad: float32 [2048, 5632], P('dp', 'mp')
- up_weight_grad: float32 [2048, 5632], P('dp', 'mp')
- down_weight_grad: float32 [5632, 2048], P('mp', 'dp')
Inputs may be any that keep to these rules, and one draw needn't show every extreme that they name: Within each row of segment_ids the numbers never fall; each number covers 1 to 256 positions of a row, and one covers exactly 256.
All inputs are finite; a program needn't handle non-finite values.
Results may differ from a plain program's by a relative error of at most 0.017.
The roundings to bfloat16 on the way count: a program that leaves them out, or rounds other values in their place, can miss the bound.
Values may be sent and summed in bfloat16 or wider, within the bound.
A program may use at most 320 MiB of HBM per device.

v0:
```python
import functools

import jax
import jax.numpy as jnp
from jax import lax
from jax.experimental import pallas as pl
from jax.experimental.pallas import tpu as pltpu
from jax.sharding import PartitionSpec as P


HEAD_DIM = 64
ROT = 16


NEG = -1e30
EPS = 1e-05
BASE = 10000.0

MESH = pl.DeviceIdType.MESH
VMEM_LIMIT = 60 * 1024 * 1024


def chip_at(spot, chips):
    side = spot // (chips // 2)
    return (spot + side * (chips - 1 - 2 * spot)) * 2 + side


def span(start, size):
    return pl.ds(pl.multiple_of(start, size), size)


def remote(src, dst, send, recv, who):
    return pltpu.make_async_remote_copy(
        src_ref=src,
        dst_ref=dst,
        send_sem=send,
        recv_sem=recv,
        device_id={"dp": who},
        device_id_type=MESH,
    )


def ring_kernel(chips, gathers, swaps, groups, *refs):
    refs = list(refs)
    scatters = sum(groups)

    def take(number):
        taken = refs[:number]
        del refs[:number]
        return taken

    shards, sends, parts = take(gathers), take(swaps), take(scatters)
    fulls, gets, grouped = take(gathers), take(swaps), take(len(groups))
    outs = []
    for group, out in zip(groups, grouped):
        outs += [out] if group == 1 else [out.at[j] for j in range(group)]
    mine, pair, ring, last = take(scatters), take(scatters), take(scatters), take(scatters)
    if gathers:
        keep_sem, give_sem, got_sem, lend_sem, lent_sem = take(5)
    if swaps:
        swap_send, swap_recv = take(2)
    if scatters:
        load_sem, pair_send, pair_recv, send_sem, recv_sem, last_send, last_recv = take(7)
    device = lax.axis_index("dp")
    chip, core = device // 2, device % 2
    row, side = chip // 2, chip % 2
    spot, way = row + side * (chips - 1 - 2 * row), 1 - 2 * core
    partner = device + way
    after = chip_at((spot + 1) % chips, chips)
    before = chip_at((spot + chips - 1) % chips, chips)
    source = chip_at((spot + chips - way) % chips, chips)
    target = chip_at((spot + chips + way) % chips, chips) * 2 + core
    barrier = pltpu.get_barrier_semaphore()
    for who in (source * 2, source * 2 + 1, partner):
        pl.semaphore_signal(barrier, inc=1, device_id={"dp": who}, device_id_type=MESH)
    if swaps:
        other = 1 - lax.axis_index("mp")
        pl.semaphore_signal(barrier, inc=1, device_id={"mp": other}, device_id_type=MESH)
    pl.semaphore_wait(barrier, 4 if swaps else 3)
    ends = []

    def begin(copy, end):
        copy.start()
        ends.append(end)
        return copy

    for i in range(swaps):
        copy = pltpu.make_async_remote_copy(
            src_ref=sends[i],
            dst_ref=gets[i],
            send_sem=swap_send.at[i],
            recv_sem=swap_recv.at[i],
            device_id={"mp": other},
            device_id_type=MESH,
        )
        begin(copy, copy.wait)
    for i in range(gathers):
        unit, cols = shards[i].shape[0], shards[i].shape[1] // 2
        own = fulls[i].at[span(device * unit, unit), :]
        for half, who in ((0, after * 2), (1, before * 2 + 1)):
            copy = remote(
                shards[i].at[:, pl.ds(half * cols, cols)],
                fulls[i].at[span(device * unit, unit), pl.ds(half * cols, cols)],
                give_sem.at[i, half],
                got_sem.at[i, core],
                who,
            )
            begin(copy, copy.wait_send)
        copy = remote(shards[i], own, lend_sem.at[i, 0], lent_sem.at[i, 0], partner)
        begin(copy, copy.wait)
        copy = pltpu.make_async_copy(shards[i], own, keep_sem.at[i])
        begin(copy, copy.wait)

    loads, pairs = {}, {}
    for step in range(chips):
        away = chip_at((spot + 2 * chips + way * (step + 1)) % chips, chips)
        here = chip_at((spot + 2 * chips - way * (step + 1)) % chips, chips)
        for i in range(scatters):
            rows, cols = mine[i].shape[1:]
            copy = remote(
                parts[i].at[span(away * rows, rows), span((1 - core) * cols, cols)],
                pair[i].at[step],
                pair_send.at[i, step],
                pair_recv.at[i, step],
                partner,
            )
            pairs[step, i] = begin(copy, copy.wait_send)
            loads[step, i] = pltpu.make_async_copy(
                parts[i].at[span(here * rows, rows), span(core * cols, cols)],
                mine[i].at[step],
                load_sem.at[i, step],
            )
            loads[step, i].start()

    def gather_step(i, step):
        held = chip_at((spot + 2 * chips - way * step) % chips, chips)
        unit, cols = shards[i].shape[0], shards[i].shape[1] // 2
        block = fulls[i].at[span(held * 2 * unit, 2 * unit), span(core * cols, cols)]
        if step == 1:
            for sender in range(2):
                piece = fulls[i].at[span((held * 2 + sender) * unit, unit), span(core * cols, cols)]
                remote(piece, piece, give_sem.at[i, 0], got_sem.at[i, sender], target).wait_recv()
        else:
            remote(block, block, give_sem.at[i, 0], got_sem.at[i, step], target).wait_recv()
        if step < chips - 1:
            copy = remote(block, block, give_sem.at[i, step + 1], got_sem.at[i, step + 1], target)
            begin(copy, copy.wait_send)
        copy = remote(block, block, lend_sem.at[i, step], lent_sem.at[i, step], partner)
        begin(copy, copy.wait)

    def scatter_step(i, step):
        rows, cols = mine[i].shape[1:]
        lines = min(rows, 32)
        loads[step, i].wait()
        pairs[step, i].wait_recv()
        if step > 0:
            came = ring[i].at[step - 1]
            remote(came, came, send_sem.at[i, 0], recv_sem.at[i, step - 1], target).wait_recv()

        @pl.loop(0, rows // lines)
        def _(k):
            at = span(k * lines, lines)
            total = mine[i][step, at, :].astype(jnp.float32)
            total = total + pair[i][step, at, :].astype(jnp.float32)
            if step > 0:
                total = total + ring[i][step - 1, at, :].astype(jnp.float32)
            if step < chips - 1:
                mine[i][step, at, :] = total.astype(jnp.bfloat16)
            else:
                last[i][at, :] = total

        if step < chips - 1:
            copy = remote(
                mine[i].at[step], ring[i].at[step], send_sem.at[i, step], recv_sem.at[i, step], target
            )
            begin(copy, copy.wait_send)
        else:
            unit = rows // 2
            place = outs[i].at[:, span(core * cols, cols)]
            copy = remote(
                last[i].at[span((1 - core) * unit, unit), :],
                place,
                last_send.at[i, 0],
                last_recv.at[i],
                partner,
            )
            begin(copy, copy.wait)
            copy = pltpu.make_async_copy(
                last[i].at[span(core * unit, unit), :], place, last_send.at[i, 1]
            )
            begin(copy, copy.wait)

    for step in range(chips):
        for i in range(gathers):
            if step > 0:
                gather_step(i, step)
        for i in range(scatters):
            scatter_step(i, step)
    for end in ends:
        end()


def ring_call(call_id, shards=(), sends=(), parts=(), groups=()):
    size = lax.axis_size("dp")
    chips = size // 2
    gathers, swaps, scatters = len(shards), len(sends), len(parts)
    outs = [jax.ShapeDtypeStruct((s.shape[0] * size, s.shape[1]), s.dtype) for s in shards]
    outs += [jax.ShapeDtypeStruct(s.shape, s.dtype) for s in sends]
    first = 0
    for group in groups:
        shape = (parts[first].shape[0] // size, parts[first].shape[1])
        outs.append(jax.ShapeDtypeStruct(shape if group == 1 else (group,) + shape, jnp.float32))
        first += group
    blocks = [(p.shape[0] // chips, p.shape[1] // 2) for p in parts]
    scratch = [pltpu.VMEM((chips,) + b, jnp.bfloat16) for b in blocks] * 2
    scratch += [pltpu.VMEM((chips - 1,) + b, jnp.bfloat16) for b in blocks]
    scratch += [pltpu.VMEM(b, jnp.float32) for b in blocks]
    if gathers:
        scratch += [pltpu.SemaphoreType.DMA((gathers,))]
        scratch += [pltpu.SemaphoreType.DMA((gathers, chips))] * 4
    if swaps:
        scratch += [pltpu.SemaphoreType.DMA((swaps,))] * 2
    if scatters:
        scratch += [pltpu.SemaphoreType.DMA((scatters, chips))] * 5
        scratch += [pltpu.SemaphoreType.DMA((scatters, 2)), pltpu.SemaphoreType.DMA((scatters,))]
    moved = sum(s.size * 2 * size for s in shards) + sum(p.size * 2 for p in parts)
    return list(
        pl.pallas_call(
            functools.partial(ring_kernel, chips, gathers, swaps, tuple(groups)),
            out_shape=outs,
            in_specs=[pl.BlockSpec(memory_space=pltpu.VMEM)] * gathers
            + [pl.BlockSpec(memory_space=pl.ANY)] * (swaps + scatters),
            out_specs=[pl.BlockSpec(memory_space=pl.ANY)] * len(outs),
            scratch_shapes=scratch,
            compiler_params=pltpu.CompilerParams(
                collective_id=call_id, has_side_effects=True, vmem_limit_bytes=VMEM_LIMIT
            ),
            cost_estimate=pl.CostEstimate(flops=0, bytes_accessed=moved, transcendentals=0),
        )(*shards, *sends, *parts)
    )


def feed_kernel(
    chips,
    tile,
    up_shard,
    down_shard,
    normed_ref,
    cot_ref,
    gate_full,
    up_full,
    down_full,
    rows_out,
    gate_out,
    up_out,
    hidden_out,
    term_out,
    rows,
    weights,
    gates,
    ups,
    hiddens,
    terms,
    keep_sem,
    give_sem,
    got_sem,
    lend_sem,
    lent_sem,
    swap_sem,
    load_sem,
    gate_sem,
    up_sem,
    hidden_sem,
    term_sem,
):
    device = lax.axis_index("dp")
    chip, core = device // 2, device % 2
    row, side = chip // 2, chip % 2
    spot, way = row + side * (chips - 1 - 2 * row), 1 - 2 * core
    partner = device + way
    after = chip_at((spot + 1) % chips, chips)
    before = chip_at((spot + chips - 1) % chips, chips)
    source = chip_at((spot + chips - way) % chips, chips)
    target = chip_at((spot + chips + way) % chips, chips) * 2 + core
    other = 1 - lax.axis_index("mp")
    barrier = pltpu.get_barrier_semaphore()
    for who in (source * 2, source * 2 + 1, partner):
        pl.semaphore_signal(barrier, inc=1, device_id={"dp": who}, device_id_type=MESH)
    pl.semaphore_signal(barrier, inc=1, device_id={"mp": other}, device_id_type=MESH)
    pl.semaphore_wait(barrier, 4)

    unit, wide = up_shard.shape
    tiles = wide // tile
    first = (wide // 256 + 1) // 2 * 256
    columns = (pl.ds(0, first), pl.ds(first, wide - first))
    shards = [ref.at[:, at] for ref in (up_shard, down_shard) for at in columns]
    fulls = [ref.at[:, at] for ref in (up_full, down_full) for at in columns]
    halves = [first // 2, (wide - first) // 2] * 2
    half_rows = normed_ref.shape[0]

    def own(i, half):
        at = slice(None) if half is None else pl.ds(half * halves[i], halves[i])
        return shards[i].at[:, at], fulls[i].at[span(device * unit, unit), at]

    def sent(i):
        copies = []
        for half, who in ((0, after * 2), (1, before * 2 + 1)):
            src, dst = own(i, half)
            copies.append(remote(src, dst, give_sem.at[i, half], got_sem.at[i, 1], who))
        return copies

    def shared(i):
        src, dst = own(i, None)
        return [
            remote(src, dst, lend_sem.at[i, 0], lent_sem.at[i, 0], partner),
            pltpu.make_async_copy(src, dst, keep_sem.at[i]),
        ]

    def block(i, step):
        held = chip_at((spot + 2 * chips - way * step) % chips, chips)
        return fulls[i].at[span(held * 2 * unit, 2 * unit), span(core * halves[i], halves[i])]

    def passed(i, step):
        at = block(i, step)
        return remote(at, at, give_sem.at[i, step + 1], got_sem.at[i, step + 1], target)

    def lent(i, step):
        at = block(i, step)
        return remote(at, at, lend_sem.at[i, step], lent_sem.at[i, step], partner)

    def relay(i, step):
        at = block(i, step)
        remote(at, at, give_sem.at[i, 0], got_sem.at[i, step], target).wait_recv()

        @pl.when(step < chips - 1)
        def _():
            passed(i, step).start()

        lent(i, step).start()

    def settle(i):
        for copy in shared(i):
            copy.wait()
        for copy in sent(i):
            copy.wait_send()

        @pl.loop(1, chips)
        def _(step):
            lent(i, step).wait()

            @pl.when(step < chips - 1)
            def _():
                passed(i, step).wait_send()

    exchange = pltpu.make_async_remote_copy(
        src_ref=normed_ref,
        dst_ref=rows.at[pl.ds(half_rows, half_rows), :],
        send_sem=swap_sem.at[0],
        recv_sem=swap_sem.at[1],
        device_id={"mp": other},
        device_id_type=MESH,
    )
    place = pltpu.make_async_copy(normed_ref, rows.at[pl.ds(0, half_rows), :], swap_sem.at[2])
    record = pltpu.make_async_copy(rows, rows_out, swap_sem.at[3])

    def load(ref, t):
        return pltpu.make_async_copy(
            ref.at[:, span(t * tile, tile)], weights.at[t % 2], load_sem.at[t % 2]
        )

    def store(buffer, out, sem, t):
        at = span(t * tile, tile)
        return pltpu.make_async_copy(buffer.at[:, at], out.at[:, at], sem.at[t])

    def store_term(t):
        return pltpu.make_async_copy(
            terms.at[t % 2], term_out.at[:, span(t * tile, tile)], term_sem.at[t % 2]
        )

    def weight_of(ref, t):
        load(ref, t).wait()

        @pl.when(t + 1 < tiles)
        def _():
            load(ref, t + 1).start()

        return weights[t % 2]

    def gate_tile(t):
        gates[:, span(t * tile, tile)] = jnp.dot(
            rows[...], weight_of(gate_full, t), preferred_element_type=jnp.float32
        )
        store(gates, gate_out, gate_sem, t).start()

    def up_tile(t):
        at = span(t * tile, tile)
        upward = jnp.dot(rows[...], weight_of(up_full, t), preferred_element_type=jnp.float32)
        ups[:, at] = upward
        store(ups, up_out, up_sem, t).start()
        gate = gates[:, at]
        hidden = (gate * jax.nn.sigmoid(gate) * upward).astype(jnp.bfloat16)
        hiddens[:, at] = hidden
        store(hiddens, hidden_out, hidden_sem, t).start()

        @pl.when(t > 1)
        def _():
            store_term(t - 2).wait()

        terms[t % 2] = jnp.dot(
            cot_ref[...], hidden, preferred_element_type=jnp.float32
        ).astype(jnp.bfloat16)
        store_term(t).start()

    def some(number, start, work):
        @pl.loop(0, number)
        def _(k):
            @pl.when(start + k < tiles)
            def _():
                work(start + k)

    for i in (0, 1):
        for copy in sent(i) + shared(i):
            copy.start()
    exchange.start()
    place.start()
    load(gate_full, 0).start()
    late = chips // 2
    each = -(-tiles // (chips - late))

    @pl.loop(1, chips)
    def _(step):
        relay(0, step)
        relay(1, step)

        @pl.when(step == chips - 2)
        def _():
            for i in (2, 3):
                for copy in sent(i) + shared(i):
                    copy.start()

        @pl.when(step == late)
        def _():
            place.wait()
            exchange.wait()
            record.start()

        @pl.when(step >= late)
        def _():
            some(each, (step - late) * each, gate_tile)

    settle(0)
    settle(1)
    load(up_full, 0).start()
    each = -(-tiles // (chips - 1))
    early = -(-each // 2)

    @pl.loop(1, chips)
    def _(step):
        relay(2, step)
        some(early, (step - 1) * each, up_tile)
        relay(3, step)
        if each > early:
            some(each - early, (step - 1) * each + early, up_tile)

    settle(2)
    settle(3)
    record.wait()

    @pl.loop(0, tiles)
    def _(t):
        store(gates, gate_out, gate_sem, t).wait()
        store(ups, up_out, up_sem, t).wait()
        store(hiddens, hidden_out, hidden_sem, t).wait()

    for t in range(max(tiles - 2, 0), tiles):
        store_term(t).wait()


def feed_call(call_id, up_shard, down_shard, normed_here, cot_turned, gate_full):
    size = lax.axis_size("dp")
    chips = size // 2
    _, wide = up_shard.shape
    depth, tokens = cot_turned.shape
    tile = 256
    tiles = wide // tile
    low, high = jnp.bfloat16, jnp.float32
    kept = pl.BlockSpec(memory_space=pltpu.VMEM)
    far = pl.BlockSpec(memory_space=pl.ANY)
    dma = pltpu.SemaphoreType.DMA
    return pl.pallas_call(
        functools.partial(feed_kernel, chips, tile),
        out_shape=[
            jax.ShapeDtypeStruct((depth, wide), low),
            jax.ShapeDtypeStruct((depth, wide), low),
            jax.ShapeDtypeStruct((tokens, depth), low),
            jax.ShapeDtypeStruct((tokens, wide), high),
            jax.ShapeDtypeStruct((tokens, wide), high),
            jax.ShapeDtypeStruct((tokens, wide), low),
            jax.ShapeDtypeStruct((depth, wide), low),
        ],
        in_specs=[kept, kept, kept, kept, far],
        out_specs=[far] * 7,
        scratch_shapes=[
            pltpu.VMEM((tokens, depth), low),
            pltpu.VMEM((2, depth, tile), low),
            pltpu.VMEM((tokens, wide), high),
            pltpu.VMEM((tokens, wide), high),
            pltpu.VMEM((tokens, wide), low),
            pltpu.VMEM((2, depth, tile), low),
            dma((4,)),
        ]
        + [dma((4, chips + 1))] * 4
        + [dma((4,)), dma((2,)), dma((tiles,)), dma((tiles,)), dma((tiles,)), dma((2,))],
        compiler_params=pltpu.CompilerParams(
            collective_id=call_id, has_side_effects=True, vmem_limit_bytes=VMEM_LIMIT
        ),
        cost_estimate=pl.CostEstimate(
            flops=6 * tokens * depth * wide,
            bytes_accessed=12 * depth * wide + 12 * tokens * wide,
            transcendentals=tokens * wide,
        ),
    )(up_shard, down_shard, normed_here, cot_turned, gate_full)


def back_kernel(
    chips,
    tile,
    cot_ref,
    normed_ref,
    gate_ref,
    up_ref,
    gate_full,
    up_full,
    down_full,
    term_ref,
    gate_out,
    up_out,
    part_out,
    far_out,
    grad_out,
    gate_term_out,
    mine_a,
    mine_b,
    pair_a,
    pair_b,
    ring_a,
    ring_b,
    last_a,
    last_b,
    weights,
    states,
    acts,
    total,
    low,
    turned,
    kept,
    terms,
    load_sem,
    state_sem,
    act_sem,
    term_sem,
    keep_sem,
    swap_sem,
    own_sem,
    pair_send,
    pair_recv,
    send_sem,
    recv_sem,
    last_send,
    last_recv,
):
    device = lax.axis_index("dp")
    chip, core = device // 2, device % 2
    row, side = chip // 2, chip % 2
    spot, way = row + side * (chips - 1 - 2 * row), 1 - 2 * core
    partner = device + way
    source = chip_at((spot + chips - way) % chips, chips)
    target = chip_at((spot + chips + way) % chips, chips) * 2 + core
    other = 1 - lax.axis_index("mp")
    barrier = pltpu.get_barrier_semaphore()
    for who in (source * 2, source * 2 + 1, partner):
        pl.semaphore_signal(barrier, inc=1, device_id={"dp": who}, device_id_type=MESH)
    pl.semaphore_signal(barrier, inc=1, device_id={"mp": other}, device_id_type=MESH)
    pl.semaphore_wait(barrier, 4)

    mine, pair, ring, last = (mine_a, mine_b), (pair_a, pair_b), (ring_a, ring_b), (last_a, last_b)
    wide = gate_ref.shape[1]
    half_rows = part_out.shape[0]
    tiles = wide // tile
    first = (wide // 256 + 1) // 2 * 256
    columns = (pl.ds(0, first), pl.ds(first, wide - first))
    parts = [term_ref.at[:, at] for at in columns]
    outs = [grad_out.at[:, at] for at in columns]

    def own(i, step):
        rows, cols = mine[i].shape[1:]
        here = chip_at((spot + 2 * chips - way * (step + 1)) % chips, chips)
        return pltpu.make_async_copy(
            parts[i].at[span(here * rows, rows), span(core * cols, cols)],
            mine[i].at[step],
            own_sem.at[i, step],
        )

    def trade(i, step):
        rows, cols = mine[i].shape[1:]
        away = chip_at((spot + 2 * chips + way * (step + 1)) % chips, chips)
        return remote(
            parts[i].at[span(away * rows, rows), span((1 - core) * cols, cols)],
            pair[i].at[step],
            pair_send.at[i, step],
            pair_recv.at[i, step],
            partner,
        )

    def onward(i, step):
        return remote(
            mine[i].at[step], ring[i].at[step], send_sem.at[i, step], recv_sem.at[i, step], target
        )

    def ending(i):
        rows, cols = mine[i].shape[1:]
        unit = rows // 2
        place = outs[i].at[:, span(core * cols, cols)]
        return (
            remote(
                last[i].at[span((1 - core) * unit, unit), :],
                place,
                last_send.at[i, 0],
                last_recv.at[i],
                partner,
            ),
            pltpu.make_async_copy(
                last[i].at[span(core * unit, unit), :], place, last_send.at[i, 1]
            ),
        )

    def sum_step(i, step):
        rows = mine[i].shape[1]
        lines = min(rows, 32)
        own(i, step).wait()
        trade(i, step).wait_recv()

        def added(at):
            value = mine[i][step, at, :].astype(jnp.float32)
            return value + pair[i][step, at, :].astype(jnp.float32)

        @pl.when(step == 0)
        def _():
            @pl.loop(0, rows // lines)
            def _(k):
                at = span(k * lines, lines)
                mine[i][step, at, :] = added(at).astype(jnp.bfloat16)

        @pl.when(step > 0)
        def _():
            came = ring[i].at[step - 1]
            remote(came, came, send_sem.at[i, 0], recv_sem.at[i, step - 1], target).wait_recv()

            @pl.when(step < chips - 1)
            def _():
                @pl.loop(0, rows // lines)
                def _(k):
                    at = span(k * lines, lines)
                    value = added(at) + ring[i][step - 1, at, :].astype(jnp.float32)
                    mine[i][step, at, :] = value.astype(jnp.bfloat16)

            @pl.when(step == chips - 1)
            def _():
                @pl.loop(0, rows // lines)
                def _(k):
                    at = span(k * lines, lines)
                    last[i][at, :] = added(at) + ring[i][step - 1, at, :].astype(jnp.float32)

        @pl.when(step < chips - 1)
        def _():
            onward(i, step).start()

        @pl.when(step == chips - 1)
        def _():
            for copy in ending(i):
                copy.start()

    def loads(t):
        at, slot = span(t * tile, tile), t % 2
        copies = [
            pltpu.make_async_copy(ref.at[:, at], weights.at[k, slot], load_sem.at[k, slot])
            for k, ref in enumerate((down_full, gate_full, up_full))
        ]
        return copies + [
            pltpu.make_async_copy(ref.at[:, at], states.at[k, slot], state_sem.at[k, slot])
            for k, ref in enumerate((gate_ref, up_ref))
        ]

    def stores(t):
        at, slot = span(t * tile, tile), t % 2
        return [
            pltpu.make_async_copy(acts.at[k, slot], ref.at[:, at], act_sem.at[k, slot])
            for k, ref in enumerate((gate_out, up_out))
        ]

    def work(t):
        slot = t % 2
        for copy in loads(t):
            copy.wait()

        @pl.when(t + 1 < tiles)
        def _():
            for copy in loads(t + 1):
                copy.start()

        @pl.when(t > 1)
        def _():
            for copy in stores(t - 2):
                copy.wait()

        hidden_grad = jnp.dot(
            cot_ref[...], weights[0, slot], preferred_element_type=jnp.float32
        )
        gate, upward = states[0, slot], states[1, slot]
        sigma = jax.nn.sigmoid(gate)
        gate_act = hidden_grad * upward * sigma * (1.0 + gate * (1.0 - sigma))
        gate_low = gate_act.astype(jnp.bfloat16)
        acts[0, slot] = gate_low
        kept[:, span(t * tile, tile)] = gate_low
        acts[1, slot] = (hidden_grad * gate * sigma).astype(jnp.bfloat16)
        for copy in stores(t):
            copy.start()
        depth = total.shape[1]
        band = depth // 4

        @pl.loop(0, 4)
        def _(k):
            at = span(k * band, band)
            value = total[:, at]
            for which in range(2):
                value = value + lax.dot_general(
                    acts[which, slot],
                    weights[which + 1, slot, at, :],
                    (((1,), (1,)), ((), ())),
                    preferred_element_type=jnp.float32,
                )
            total[:, at] = value

    def store_term(t):
        return pltpu.make_async_copy(
            terms.at[t % 2], gate_term_out.at[:, span(t * tile, tile)], term_sem.at[t % 2]
        )

    def term_work(t):
        @pl.when(t > 1)
        def _():
            store_term(t - 2).wait()

        terms[t % 2] = jnp.dot(
            turned[...], kept[:, span(t * tile, tile)], preferred_element_type=jnp.float32
        ).astype(jnp.bfloat16)
        store_term(t).start()

    def some(number, start, task):
        @pl.loop(0, number)
        def _(k):
            @pl.when((start + k >= 0) & (start + k < tiles))
            def _():
                task(start + k)

    keep = pltpu.make_async_copy(total.at[pl.ds(0, half_rows), :], part_out, keep_sem.at[0])
    exchange = pltpu.make_async_remote_copy(
        src_ref=low,
        dst_ref=far_out,
        send_sem=swap_sem.at[0],
        recv_sem=swap_sem.at[1],
        device_id={"mp": other},
        device_id_type=MESH,
    )

    @pl.loop(0, chips)
    def _(step):
        for i in range(2):
            trade(i, step).start()
            own(i, step).start()

    for copy in loads(0):
        copy.start()
    total[...] = jnp.zeros_like(total)

    @pl.loop(0, normed_ref.shape[1] // 256)
    def _(k):
        turned[span(k * 256, 256), :] = normed_ref[:, span(k * 256, 256)].T

    each = -(-tiles // (chips - 1))
    early = -(-each // 2)
    done = -(-tiles // each)
    rest = -(-tiles // (chips - done))
    half_rest = -(-rest // 2)

    @pl.loop(0, chips)
    def _(step):
        sum_step(0, step)
        some(early, step * each, work)

        @pl.when(step >= done)
        def _():
            some(half_rest, (step - done) * rest, term_work)

        sum_step(1, step)
        if each > early:
            some(each - early, step * each + early, work)
        if rest > half_rest:

            @pl.when(step >= done)
            def _():
                some(rest - half_rest, (step - done) * rest + half_rest, term_work)

        @pl.when(step == done - 1)
        def _():
            low[...] = total[pl.ds(half_rows, half_rows), :].astype(jnp.bfloat16)
            exchange.start()
            keep.start()

    keep.wait()
    exchange.wait()
    for t in range(max(tiles - 2, 0), tiles):
        for copy in stores(t):
            copy.wait()
        store_term(t).wait()
    for i in range(2):
        for copy in ending(i):
            copy.wait()

    @pl.loop(0, chips)
    def _(step):
        for i in range(2):
            trade(i, step).wait_send()

            @pl.when(step < chips - 1)
            def _():
                onward(i, step).wait_send()


def back_call(call_id, cot_rows, normed_two, gate, upward, gate_full, up_full, down_full, down_term):
    size = lax.axis_size("dp")
    chips = size // 2
    tokens, depth = cot_rows.shape
    wide = gate.shape[1]
    tile = 256
    first = (wide // 256 + 1) // 2 * 256
    blocks = [(depth // chips, first // 2), (depth // chips, (wide - first) // 2)]
    low, high = jnp.bfloat16, jnp.float32
    far = pl.BlockSpec(memory_space=pl.ANY)
    dma = pltpu.SemaphoreType.DMA
    return pl.pallas_call(
        functools.partial(back_kernel, chips, tile),
        out_shape=[
            jax.ShapeDtypeStruct((tokens, wide), low),
            jax.ShapeDtypeStruct((tokens, wide), low),
            jax.ShapeDtypeStruct((tokens // 2, depth), high),
            jax.ShapeDtypeStruct((tokens // 2, depth), low),
            jax.ShapeDtypeStruct((depth // size, wide), high),
            jax.ShapeDtypeStruct((depth, wide), low),
        ],
        in_specs=[pl.BlockSpec(memory_space=pltpu.VMEM)] * 2 + [far] * 6,
        out_specs=[far] * 6,
        scratch_shapes=[pltpu.VMEM((chips,) + b, low) for b in blocks] * 2
        + [pltpu.VMEM((chips - 1,) + b, low) for b in blocks]
        + [pltpu.VMEM(b, high) for b in blocks]
        + [
            pltpu.VMEM((3, 2, depth, tile), low),
            pltpu.VMEM((2, 2, tokens, tile), high),
            pltpu.VMEM((2, 2, tokens, tile), low),
            pltpu.VMEM((tokens, depth), high),
            pltpu.VMEM((tokens // 2, depth), low),
            pltpu.VMEM((depth, tokens), low),
            pltpu.VMEM((tokens, wide), low),
            pltpu.VMEM((2, depth, tile), low),
            dma((3, 2)),
            dma((2, 2)),
            dma((2, 2)),
            dma((2,)),
            dma((1,)),
            dma((2,)),
        ]
        + [dma((2, chips))] * 5
        + [dma((2, 2)), dma((2,))],
        compiler_params=pltpu.CompilerParams(
            collective_id=call_id, has_side_effects=True, vmem_limit_bytes=VMEM_LIMIT
        ),
        cost_estimate=pl.CostEstimate(
            flops=8 * tokens * depth * wide,
            bytes_accessed=8 * depth * wide + 12 * tokens * wide,
            transcendentals=tokens * wide,
        ),
    )(cot_rows, normed_two, gate, upward, gate_full, up_full, down_full, down_term)


def layer_norm(values, norm_gain, norm_shift):
    center = values - jnp.mean(values, axis=-1, keepdims=True)
    inverse = lax.rsqrt(jnp.mean(center * center, axis=-1, keepdims=True) + EPS)
    scaled = center * inverse
    return (scaled * norm_gain + norm_shift, scaled, inverse)


def norm_back(grads, scaled, inverse, norm_gain):
    weighted = grads * norm_gain
    return inverse * (
        weighted
        - jnp.mean(weighted, axis=-1, keepdims=True)
        - scaled * jnp.mean(weighted * scaled, axis=-1, keepdims=True)
    )


def rotary_tables(segments, places, rotary_dims):
    earlier = (segments[None, :] < segments[:, None]).astype(jnp.int32)
    position = (places - jnp.sum(earlier, axis=1)).astype(jnp.float32)
    half_dims = rotary_dims // 2
    frequency = BASE ** (-2.0 * jnp.arange(half_dims, dtype=jnp.float32) / rotary_dims)
    angles = position[:, None] * frequency[None, :]
    return (jnp.cos(angles), jnp.sin(angles))


def rotate(values, cosine, sine_table, rotary_dims, turn_sign):
    half_dims = rotary_dims // 2
    leading = values[..., :half_dims]
    trailing = values[..., half_dims:rotary_dims]
    cos_rows = cosine[:, None, :]
    sin_rows = turn_sign * sine_table[:, None, :]
    return jnp.concatenate(
        [
            leading * cos_rows - trailing * sin_rows,
            trailing * cos_rows + leading * sin_rows,
            values[..., rotary_dims:],
        ],
        axis=-1,
    )


def masked_scores(query, key_rot, allowed, score_scale):
    scores = (
        jnp.einsum("qhd,khd->hqk", query, key_rot, preferred_element_type=jnp.float32) * score_scale
    )
    return jnp.where(allowed[None], scores, NEG)


def swap(values):
    return lax.ppermute(values, "mp", [(0, 1), (1, 0)])


def half_sum(part):
    half = part.shape[0] // 2
    other = swap(part[half:].astype(jnp.bfloat16))
    return part[:half] + other.astype(jnp.float32)


def grow(rows):
    return jnp.concatenate([rows, swap(rows)], axis=0)


def scatter(term, axis):
    return lax.psum_scatter(term, "dp", scatter_dimension=axis, tiled=True).astype(jnp.float32)


def body(
    inputs,
    segment_ids,
    norm1_gain,
    norm1_shift,
    qkv_weight,
    qkv_bias,
    out_weight,
    norm2_gain,
    norm2_shift,
    gate_weight,
    up_weight,
    down_weight,
    cotangent,
):
    score_scale = HEAD_DIM ** (-0.5)
    rows_here = inputs.shape[0]
    width = inputs.shape[1]
    *qkv_full, out_turned, far_inputs, far_cot = ring_call(
        0,
        shards=[qkv_weight[0], qkv_weight[1], qkv_weight[2], out_weight.T],
        sends=[inputs, cotangent],
    )
    input_rows = jnp.concatenate([inputs, far_inputs], axis=0)
    cot_rows = jnp.concatenate([cotangent, far_cot], axis=0)
    gate_weight, out_turned = lax.optimization_barrier((gate_weight, out_turned))
    gate_full = lax.all_gather(gate_weight, "dp", axis=0, tiled=True)
    stream_rows = input_rows.astype(jnp.float32)
    stream = stream_rows[:rows_here]
    normed_wide, scaled_rows, inverse_rows = layer_norm(stream_rows, norm1_gain, norm1_shift)
    normed_one = normed_wide.astype(jnp.bfloat16)
    scaled_one = scaled_rows[:rows_here]
    inverse_one = inverse_rows[:rows_here]
    seq_len = normed_one.shape[0]
    local_width = qkv_full[0].shape[1]
    head_count = local_width // HEAD_DIM
    turn = lax.axis_index("mp") * rows_here
    segments = jnp.roll(segment_ids[0], -turn)
    places = jnp.roll(jnp.arange(seq_len, dtype=jnp.int32), -turn)
    allowed = (places[None, :] <= places[:, None]) & (segments[:, None] == segments[None, :])
    cosine, sine_table = rotary_tables(segments, places, ROT)
    shaped = [
        (jnp.dot(normed_one, full, preferred_element_type=jnp.float32) + bias).reshape(
            seq_len, head_count, HEAD_DIM
        )
        for full, bias in zip(qkv_full, qkv_bias)
    ]
    query = rotate(shaped[0], cosine, sine_table, ROT, 1.0).astype(jnp.bfloat16)
    key_rot = rotate(shaped[1], cosine, sine_table, ROT, 1.0).astype(jnp.bfloat16)
    value = shaped[2].astype(jnp.bfloat16)
    scores = masked_scores(query, key_rot, allowed, score_scale)
    row_max = jnp.max(scores, axis=-1, keepdims=True)
    exponent = jnp.exp(scores - row_max)
    row_total = jnp.sum(exponent, axis=-1, keepdims=True)
    log_total = row_max + jnp.log(row_total)
    probs_low = (exponent / row_total).astype(jnp.bfloat16)
    mixed_heads = jnp.einsum(
        "hqk,khd->qhd", probs_low, value, preferred_element_type=jnp.float32
    ).astype(jnp.bfloat16)
    mixed = mixed_heads.reshape(seq_len, local_width)
    branch = jnp.dot(mixed, out_turned.T, preferred_element_type=jnp.float32)
    middle = stream + half_sum(branch)
    normed_wide2, scaled_two, inverse_two = layer_norm(middle, norm2_gain, norm2_shift)
    normed_here = normed_wide2.astype(jnp.bfloat16)
    up_full, down_turned, normed_two, gate, upward, hidden, down_term = feed_call(
        1, up_weight, down_weight.T, normed_here, cot_rows.T, gate_full
    )
    _, up_act, part_here, part_far, down_grad_turned, gate_term = back_call(
        3, cot_rows, normed_two, gate, upward, gate_full, up_full, down_turned, down_term
    )
    down_weight_grad = down_grad_turned.T
    normed_two_grad = part_here + part_far.astype(jnp.float32)
    gate_weight_grad = scatter(gate_term, 0)
    gain_two = jnp.sum(normed_two_grad * scaled_two, axis=0)
    shift_two = jnp.sum(normed_two_grad, axis=0)
    middle_grad = cotangent.astype(jnp.float32) + norm_back(
        normed_two_grad, scaled_two, inverse_two, norm2_gain
    )
    middle_low, hidden, up_act = lax.optimization_barrier(
        (middle_grad.astype(jnp.bfloat16), hidden, up_act)
    )
    middle_rows = grow(middle_low)
    up_term = jnp.dot(normed_two.T, up_act, preferred_element_type=jnp.float32)
    feed_part = jnp.dot(hidden, down_turned.T, preferred_element_type=jnp.float32)
    out_term = jnp.dot(middle_rows.T, mixed, preferred_element_type=jnp.float32)
    mixed_grad = (
        jnp.dot(middle_rows, out_turned, preferred_element_type=jnp.float32)
        .astype(jnp.bfloat16)
        .reshape(seq_len, head_count, HEAD_DIM)
    )
    probs_wide = jnp.exp(scores - log_total)
    value_grad = jnp.einsum(
        "hqk,qhd->khd",
        probs_wide.astype(jnp.bfloat16),
        mixed_grad,
        preferred_element_type=jnp.float32,
    )
    prob_grad = jnp.einsum("qhd,khd->hqk", mixed_grad, value, preferred_element_type=jnp.float32)
    row_delta = jnp.transpose(
        jnp.sum(mixed_grad.astype(jnp.float32) * mixed_heads.astype(jnp.float32), axis=-1)
    )
    score_grad = (probs_wide * (prob_grad - row_delta[:, :, None]) * score_scale).astype(
        jnp.bfloat16
    )
    query_grad = jnp.einsum("hqk,khd->qhd", score_grad, key_rot, preferred_element_type=jnp.float32)
    key_grad = jnp.einsum("hqk,qhd->khd", score_grad, query, preferred_element_type=jnp.float32)
    query_back = rotate(query_grad, cosine, sine_table, ROT, -1.0)
    key_back = rotate(key_grad, cosine, sine_table, ROT, -1.0)
    proj_grad = [
        part.reshape(seq_len, local_width) for part in (query_back, key_back, value_grad)
    ]
    rotated_cols = jnp.arange(local_width, dtype=jnp.int32) % HEAD_DIM < ROT
    bias_sums = [jnp.sum(part, axis=0) for part in proj_grad]
    bias_term = [bias_sums[0], jnp.where(rotated_cols, bias_sums[1], 0.0), bias_sums[2]]
    proj_low = [part.astype(jnp.bfloat16) for part in proj_grad]
    normed_one_part = jnp.zeros((), jnp.float32)
    for part, full in zip(proj_low, qkv_full):
        normed_one_part = normed_one_part + jnp.dot(
            part, full.T, preferred_element_type=jnp.float32
        )
    gain_one = jnp.sum(normed_one_part * scaled_rows, axis=0)
    shift_one = jnp.sum(normed_one_part, axis=0)
    norm_sums = jnp.concatenate([gain_one, shift_one, gain_two, shift_two])
    norm_sums = norm_sums + swap(norm_sums)
    sums = jnp.concatenate([norm_sums] + bias_term)
    spare = -sums.size % (8 * 256)
    qkv_term = [
        jnp.dot(normed_one.T, part, preferred_element_type=jnp.float32) for part in proj_low
    ]
    all_sums, far_part, far_feed, up_weight_grad, out_grad_turned, qkv_weight_grad = ring_call(
        2,
        shards=[jnp.pad(sums, (0, spare)).reshape(8, -1)],
        sends=[part[rows_here:].astype(jnp.bfloat16) for part in (normed_one_part, feed_part)],
        parts=[term.astype(jnp.bfloat16) for term in [up_term, out_term] + qkv_term],
        groups=[1, 1, 3],
    )
    out_weight_grad = out_grad_turned.T
    normed_one_grad = normed_one_part[:rows_here] + far_part.astype(jnp.float32)
    feed = feed_part[:rows_here] + far_feed.astype(jnp.float32)
    output = (middle + feed).astype(jnp.bfloat16)
    all_sums = jnp.sum(all_sums.reshape(-1, 8, all_sums.shape[1]), axis=0).reshape(-1)
    gain_one, shift_one, gain_two, shift_two = all_sums[: 4 * width].reshape(4, width)
    qkv_bias_grad = all_sums[4 * width : sums.size].reshape(3, local_width)
    input_grad = middle_grad + norm_back(normed_one_grad, scaled_one, inverse_one, norm1_gain)
    return (
        output,
        input_grad,
        gain_one,
        shift_one,
        qkv_weight_grad,
        qkv_bias_grad,
        out_weight_grad,
        gain_two,
        shift_two,
        gate_weight_grad,
        up_weight_grad,
        down_weight_grad,
    )


def solution(mesh):
    in_specs = (
        P(("dp", "mp"), None),
        P("dp", None),
        P(),
        P(),
        P(None, "dp", "mp"),
        P(None, "mp"),
        P("mp", "dp"),
        P(),
        P(),
        P("dp", "mp"),
        P("dp", "mp"),
        P("mp", "dp"),
        P(("dp", "mp"), None),
    )
    out_specs = (
        P(("dp", "mp"), None),
        P(("dp", "mp"), None),
        P(),
        P(),
        P(None, "dp", "mp"),
        P(None, "mp"),
        P("mp", "dp"),
        P(),
        P(),
        P("dp", "mp"),
        P("dp", "mp"),
        P("mp", "dp"),
    )
    return jax.shard_map(body, mesh=mesh, in_specs=in_specs, out_specs=out_specs, check_vma=False)
```

profile of v0, /device:TPU:0, one launch (start us, length us, event | category | flops | bytes accessed | tf_op | source)
XLA Modules:
  0.0 690.7 jit_solution(1121204011651115129)
XLA Ops:
  9.1 2.0 slice_bitcast_fusion
  11.1 87.9 %shard_map.220 = (bf16[2048,1024]{1,0:T(8,128)(2,1)}, bf16[2048,1024]{1,0:T(8,128)(2,1)}, bf16[2048,1024]{1,0:T(8,128)(2,1)}, bf16[2048,1024]{1,0:T(8,128)(2,1)}...) custom-call(bf16[128,1024]{1,0:T(8,128)(2,1)} %get-tuple-element.119.refs_0_, ...), custom_call_target="tpu_custom_call" | custom-call | bytes 16777216 | tf_op jit(solution)/shard_map/pallas_call | solution.py:228
  101.6 5.5 add_convert_fusion.2
  107.2 2.0 copy.45
  109.2 6.3 convolution_add_fusion
  115.5 2.9 copy.47
  118.4 2.4 slice.187
  120.8 5.9 convolution_add_fusion.1
  126.7 2.9 copy.46
  129.6 2.4 slice.188
  134.8 11.1 %fusion.32 = (f32[16,512]{1,0:T(8,128)S(1)}, f32[16,512,512]{1,2,0:T(8,128)}) fusion(bf16[512,16,48]{0,2,1:T(8,128)(2,1)} %slice.187, bf16[512,16,8]{0,2,1:T(8,128)(2,1)S(1)} %get-tuple-element.127, bf16[512,16,8]{0,2,1:T(8,128)(2,1)S(1)} %get-tuple-element.128, bf16[512,16,48]{0,2,1:T(8,128)(2,1)} %slice.188, ...), kind=kOutput, calls=%fused_computation.119 | convolution fusion | flops 555737088 | bytes 19169280 | tf_op jit(solution)/shard_map/qhd,khd->hqk/dot_general | solution.py:938
  145.9 8.4 %fusion = f32[16,512]{1,0:T(8,128)S(1)} fusion(f32[16,512,512]{1,2,0:T(8,128)} %get-tuple-element.136, f32[16,512]{1,0:T(8,128)S(1)} %get-tuple-element.135), kind=kLoop, calls=%fused_computation.5 | loop fusion | flops 8380416 | bytes 16842752 | tf_op jit(solution)/shard_map/reduce_sum | solution.py:1014
  154.4 8.0 %fusion.10 = bf16[16,64,512]{2,1,0:T(8,128)(2,1)S(1)} fusion(bf16[512,16,64]{0,2,1:T(8,128)(2,1)S(1)} %bitcast.74, f32[16,512,512]{1,2,0:T(8,128)} %get-tuple-element.136, f32[16,512]{1,0:T(8,128)S(1)} %fusion, f32[16,512]{1,0:T(8,128)S(1)} %get-tuple-element.135), kind=kOutput, calls=%fused_computation.54 | convolution fusion | flops 549978112 | bytes 18939904 | tf_op jit(solution)/shard_map/hqk,khd->qhd/dot_general | solution.py:1017
  162.4 2.4 fusion.33
  164.8 1.9 copy-done.19
  169.5 2.2 copy.49
  172.7 2.3 constant_dynamic-update-slice_fusion.cot_ref
  175.0 3.9 copy.50.cot_ref
  179.5 14.0 %collective-permute-done = bf16[256,2048]{1,0:T(8,128)(2,1)} collective-permute-done((bf16[256,2048]{1,0:T(8,128)(2,1)}, bf16[256,2048]{1,0:T(8,128)(2,1)}, u32[]{:S(2)}, u32[]{:S(2)}) %collective-permute-start) | collective-permute-done | bytes 1048608 | tf_op jit(solution)/shard_map/ppermute | solution.py:944
  197.7 119.7 %shard_map.221 = (bf16[2048,2816]{1,0:T(8,128)(2,1)}, bf16[2048,2816]{1,0:T(8,128)(2,1)}, bf16[512,2048]{1,0:T(8,128)(2,1)}, f32[512,2816]{1,0:T(8,128)}, f32[51...) custom-call(bf16[128,2816]{1,0:T(8,128)(2,1)} %up_shard.1, bf16[128,2816]{1,0:T(8,128)(2,1)} %bitcast.84, ...), custom_call_target="tpu_custom_call" | custom-call | flops 17716740096 | bytes 86507520 | tf_op jit(solution)/shard_map/pallas_call | solution.py:490
  317.4 72.3 %shard_map.222 = (bf16[512,2816]{1,0:T(8,128)(2,1)}, bf16[512,2816]{1,0:T(8,128)(2,1)}, f32[256,2048]{1,0:T(8,128)}, bf16[256,2048]{1,0:T(8,128)(2,1)}, f32[128,2816]{1,0:T(8,128)}, /*index=5*/bf16[2048,2816]{1,0:T(8,128)(2,1)}) custom-call(bf16[512,2048]{1,0:T(8,128)(2,1)} %constant_dynamic-update-slice_fusion.cot_ref, ...), custom_call_target="tpu_custom_call" | custom-call | flops 23622320128 | bytes 63438848 | tf_op jit(solution)/shard_map/pallas_call | solution.py:851
  391.3 3.5 multiply_reduce_fusion.3
  395.0 2.7 fusion.27
  397.7 9.8 %fusion.34 = f32[512,2048]{1,0:T(8,128)S(1)} fusion(bf16[512,2816]{1,0:T(8,128)(2,1)S(1)} %copy-done.59, bf16[2048,2816]{1,0:T(8,128)(2,1)} %get-tuple-element.54.down_full), kind=kOutput, calls=%fused_computation.121 | convolution fusion | flops 5905580032 | bytes 18612224 | tf_op jit(solution)/shard_map/dot_general | solution.py:1044
  407.4 2.0 copy-done.18
  411.7 3.0 copy.57
  416.0 11.2 %convolution_convert_fusion.refs_3_ = bf16[2048,2816]{1,0:T(8,128)(2,1)} fusion(bf16[512,2048]{1,0:T(8,128)(2,1)} %get-tuple-element.50.normed_ref, bf16[512,2816]{1,0:T(8,128)(2,1)} %get-tuple-element.62), kind=kOutput, calls=%fused_computation.7 | convolution fusion | flops 5911347200 | bytes 16515072 | tf_op jit(solution)/shard_map/dot_general | solution.py:1043
  427.2 7.3 %collective-permute-done.1 = bf16[256,2048]{1,0:T(8,128)(2,1)} collective-permute-done((bf16[256,2048]{1,0:T(8,128)(2,1)}, bf16[256,2048]{1,0:T(8,128)(2,1)}, u32[]{:S(2)}, u32[]{:S(2)}) %collective-permute-start.1) | collective-permute-done | bytes 1048608 | tf_op jit(solution)/shard_map/ppermute | solution.py:944
  437.2 3.3 convolution_convert_fusion.5
  440.5 2.3 copy.51
  442.8 1.9 multiply_reduce_fusion.4
  444.7 11.1 %multiply_convert_fusion = bf16[16,512,512]{1,2,0:T(8,128)(2,1)S(1)} fusion(f32[16,512,512]{1,2,0:T(8,128)} %get-tuple-element.136, bf16[512,16,64]{0,2,1:T(8,128)(2,1)} %bitcast.66, bf16[512,16,64]{0,2,1:T(8,128)(2,1)} %bitcast.75, f32[16,512]{1,0:T(8,128)S(1)} %bitcast.86, f32[16,512]{1,0:T(8,128)} %log_add_fusion), kind=kOutput, calls=%fused_computation | convolution fusion | flops 557842432 | bytes 27328512 | tf_op jit(solution)/shard_map/qhd,khd->hqk/dot_general | solution.py:1058
  455.9 2.6 convolution_bitcast_fusion
  468.0 4.5 fusion.35
  472.5 4.3 fusion.36
  476.9 9.0 %bitcast_reduce_fusion = (f32[16,64]{1,0:T(8,128)S(1)}, bf16[16,64,512]{2,1,0:T(8,128)(2,1)S(1)}) fusion(bf16[512,16,64]{0,2,1:T(8,128)(2,1)S(1)} %bitcast.67, f32[16,512,512]{1,2,0:T(8,128)} %get-tuple-element.136, f32[16,512]{1,0:T(8,128)S(1)} %copy-done.32), kind=kOutput, calls=%fused_computation.34 | convolution fusion | flops 546307072 | bytes 18911232 | tf_op jit(solution)/shard_map/hqk,qhd->khd/dot_general | solution.py:1052
  485.9 8.9 %multiply_reduce_fusion = (f32[2048]{0:T(1024)S(1)}, f32[2048]{0:T(1024)S(1)}, f32[512,2048]{1,0:T(8,128)}, f32[512,2048]{1,0:T(8,128)}) fusion(f32[512]{0:T(512)S(1)} %copy-done.49, f32[512]{0:T(512)S(1)} %copy-done.45, bf16[256,2048]{1,0:T(8,128)(2,1)S(1)} %copy-done.3, bf16[256,2048]{1,0:T(8,128)(2,1)S(1)} %copy-done, ...), kind=kOutput, calls=%fused_computation.11 | convolution fusion | flops 2159013888 | bytes 24137728 | tf_op jit(solution)/shard_map/dot_general | solution.py:1078
  496.5 4.4 convolution_convert_fusion.4.refs_4_
  500.9 4.7 convolution_convert_fusion.1.refs_7_
  505.6 4.7 convolution_convert_fusion.2.refs_6_
  510.2 4.7 convolution_convert_fusion.3.refs_5_
  515.3 2.7 slice.185.refs_1_
  518.7 146.2 %shard_map.223 = (f32[128,1536]{1,0:T(8,128)}, bf16[256,2048]{1,0:T(8,128)(2,1)}, bf16[256,2048]{1,0:T(8,128)(2,1)}, f32[128,2816]{1,0:T(8,128)}, f32[128,1024]{1,0:T(8,128)}, /*index=5*/f32[3,128,1024]{2,1,0:T(8,128)}) custom-call(f32[8,1536]{1,0:T(8,128)} %reshape.269.refs_0_, bf16[256,2048]{1,0:T(8,128)(2,1)} %slice.185.refs_1_, ...), custom_call_target="tpu_custom_call" | custom-call | bytes 28704768 | tf_op jit(solution)/shard_map/pallas_call | solution.py:228
  666.8 2.0 copy.56
  668.8 3.2 fusion.15
  672.6 3.5 fusion.8
  676.8 2.0 multiply_add_fusion
  678.9 2.5 convert_element_type.142
  (184 shorter events, 41.1 us)
Async XLA Ops:
  7.2 92.0 %copy-start = (bf16[256,2048]{1,0:T(8,128)(2,1)S(1)}, bf16[256,2048]{1,0:T(8,128)(2,1)}, u32[]{:S(2)}) copy-start(bf16[256,2048]{1,0:T(8,128)(2,1)} %refs_4_.1) | copy-start | bytes 3145732
  7.2 190.5 %all-gather.2.cloned.1.call-start = ((), (), s32[]{:S(2)}) async-start(), calls=%async_computation.1 | async-start | bytes 12255232 | tf_op jit(solution)/shard_map/all_gather | solution.py:987
  99.1 579.8 %reduce-scatter.2.cloned.1.call-start = ((), (), s32[]{:S(2)}) async-start(), calls=%async_computation.2 | async-start | bytes 12255232 | tf_op jit(solution)/shard_map/reduce_scatter | solution.py:958
  100.9 19.9 %copy-start.44 = (f32[512]{0:T(512)}, f32[512]{0:T(512)S(1)}, u32[]{:S(2)}) copy-start(f32[512]{0:T(512)S(1)} %broadcast_multiply_fusion.1) | copy-start | bytes 6148
  101.6 19.2 %copy-start.48 = (f32[512]{0:T(512)}, f32[512]{0:T(512)S(1)}, u32[]{:S(2)}) copy-start(f32[512]{0:T(512)S(1)} %add_rsqrt_fusion) | copy-start | bytes 6148
  109.2 45.1 %copy-start.15 = (bf16[512,1024]{0,1:T(8,128)(2,1)}, bf16[512,1024]{0,1:T(8,128)(2,1)S(1)}, u32[]{:S(2)}) copy-start(bf16[512,1024]{0,1:T(8,128)(2,1)S(1)} %copy.45) | copy-start | bytes 3145732
  126.7 5.3 copy-start.52
  134.8 11.1 %copy-start.28 = (bf16[512,16,8]{0,2,1:T(8,128)(2,1)}, bf16[512,16,8]{0,2,1:T(8,128)(2,1)S(1)}, u32[]{:S(2)}) copy-start(bf16[512,16,8]{0,2,1:T(8,128)(2,1)S(1)} %get-tuple-element.114) | copy-start | bytes 393220
  145.9 8.4 %copy-start.33 = (f32[16,512]{1,0:T(8,128)}, f32[16,512]{1,0:T(8,128)S(1)}, u32[]{:S(2)}) copy-start(f32[16,512]{1,0:T(8,128)S(1)} %get-tuple-element.135) | copy-start | bytes 98308
  154.4 8.1 %copy-start.34 = (f32[16,512]{1,0:T(8,128)}, f32[16,512]{1,0:T(8,128)S(1)}, u32[]{:S(2)}) copy-start(f32[16,512]{1,0:T(8,128)S(1)} %fusion) | copy-start | bytes 98308
  154.4 8.0 %copy-start.55 = (bf16[2048,1024]{1,0:T(8,128)(2,1)S(1)}, bf16[2048,1024]{1,0:T(8,128)(2,1)}, u32[]{:S(2)}) copy-start(bf16[2048,1024]{1,0:T(8,128)(2,1)} %get-tuple-element.47) | copy-start | bytes 12582916
  166.8 4.9 copy-start.8
  167.9 25.6 %collective-permute-start = (bf16[256,2048]{1,0:T(8,128)(2,1)}, bf16[256,2048]{1,0:T(8,128)(2,1)}, u32[]{:S(2)}, u32[]{:S(2)}) collective-permute-start(bf16[256,2048]{1,0:T(8,128)(2,1)} %slice.186), channel_id=1, source_target_pairs={{0,1},{1,0},{2,3},{3,2},{4,5},{5,4},{6,7},{7,6},{8,9},{9,8},{10,11... | collective-permute-start | bytes 3145736 | tf_op jit(solution)/shard_map/ppermute | solution.py:944
  178.9 14.6 %copy-start.20 = (f32[512,2048]{1,0:T(8,128)S(1)}, f32[512,2048]{1,0:T(8,128)}, u32[]{:S(2)}) copy-start(f32[512,2048]{1,0:T(8,128)} %copy-done.19) | copy-start | bytes 12582916
  179.5 16.8 %copy-start.35 = (f32[2048]{0:T(1024)S(1)}, f32[2048]{0:T(1024)}, u32[]{:S(2)}) copy-start(f32[2048]{0:T(1024)} %param.22) | copy-start | bytes 24580
  179.5 16.8 %copy-start.51 = (f32[2048]{0:T(1024)S(1)}, f32[2048]{0:T(1024)}, u32[]{:S(2)}) copy-start(f32[2048]{0:T(1024)} %param.23) | copy-start | bytes 24580
  389.7 5.2 copy-start.9
  389.7 5.1 copy-start.10
  389.8 5.1 copy-start.13
  389.8 5.1 copy-start.36
  389.8 5.1 copy-start.43
  389.8 5.1 copy-start.47
  410.6 23.9 %collective-permute-start.1 = (bf16[256,2048]{1,0:T(8,128)(2,1)}, bf16[256,2048]{1,0:T(8,128)(2,1)}, u32[]{:S(2)}, u32[]{:S(2)}) collective-permute-start(bf16[256,2048]{1,0:T(8,128)(2,1)} %get-tuple-element.61), channel_id=1, source_target_pairs={{0,1},{1,0},{2,3},{3,2},{4,5},{5,4},{6,7},{7,6},{8,9},{9,8},{10,11... | collective-permute-start | bytes 3145736 | tf_op jit(solution)/shard_map/ppermute | solution.py:944
  416.0 21.2 %copy-start.56 = (bf16[2048,1024]{1,0:T(8,128)(2,1)S(1)}, bf16[2048,1024]{1,0:T(8,128)(2,1)}, u32[]{:S(2)}) copy-start(bf16[2048,1024]{1,0:T(8,128)(2,1)} %get-tuple-element.47) | copy-start | bytes 12582916
  444.7 11.1 %copy-start.17 = (bf16[512,16,48]{0,2,1:T(8,128)(2,1)S(1)}, bf16[512,16,48]{0,2,1:T(8,128)(2,1)}, u32[]{:S(2)}) copy-start(bf16[512,16,48]{0,2,1:T(8,128)(2,1)} %slice.188) | copy-start | bytes 2359300
  444.7 11.1 %copy-start.29 = (bf16[512,16,8]{0,2,1:T(8,128)(2,1)S(1)}, bf16[512,16,8]{0,2,1:T(8,128)(2,1)}, u32[]{:S(2)}) copy-start(bf16[512,16,8]{0,2,1:T(8,128)(2,1)} %copy-done.28) | copy-start | bytes 393220
  459.6 3.7 copy-start.7
  464.5 3.6 copy-start.54
  468.0 4.5 copy-start.53
  472.5 4.3 copy-start.5
  472.5 4.3 copy-start.32
  476.8 9.0 %copy-start.3 = (bf16[256,2048]{1,0:T(8,128)(2,1)S(1)}, bf16[256,2048]{1,0:T(8,128)(2,1)}, u32[]{:S(2)}) copy-start(bf16[256,2048]{1,0:T(8,128)(2,1)} %get-tuple-element.42) | copy-start | bytes 3145732
  476.8 9.0 %copy-start.14 = (bf16[2048,1024]{1,0:T(8,128)(2,1)S(1)}, bf16[2048,1024]{1,0:T(8,128)(2,1)}, u32[]{:S(2)}) copy-start(bf16[2048,1024]{1,0:T(8,128)(2,1)} %get-tuple-element.43) | copy-start | bytes 12582916
  476.9 9.0 %copy-start.45 = (f32[512]{0:T(512)S(1)}, f32[512]{0:T(512)}, u32[]{:S(2)}) copy-start(f32[512]{0:T(512)} %copy-done.44) | copy-start | bytes 6148
  476.9 9.0 %copy-start.49 = (f32[512]{0:T(512)S(1)}, f32[512]{0:T(512)}, u32[]{:S(2)}) copy-start(f32[512]{0:T(512)} %copy-done.48) | copy-start | bytes 6148
  485.9 9.0 %copy-start.37 = (f32[2048]{0:T(1024)S(1)}, f32[2048]{0:T(1024)}, u32[]{:S(2)}) copy-start(f32[2048]{0:T(1024)} %get-tuple-element.97) | copy-start | bytes 24580
  485.9 9.0 %copy-start.38 = (f32[2048]{0:T(1024)S(1)}, f32[2048]{0:T(1024)}, u32[]{:S(2)}) copy-start(f32[2048]{0:T(1024)} %get-tuple-element.102) | copy-start | bytes 24580
  485.9 10.6 %copy-start.27 = (bf16[16,64,512]{2,1,0:T(8,128)(2,1)S(1)}, bf16[16,64,512]{2,1,0:T(8,128)(2,1)}, u32[]{:S(2)}) copy-start(bf16[16,64,512]{2,1,0:T(8,128)(2,1)} %copy-done.26) | copy-start | bytes 3145732
  485.9 10.6 %copy-start.31 = (bf16[512,2048]{1,0:T(8,128)(2,1)S(1)}, bf16[512,2048]{1,0:T(8,128)(2,1)}, u32[]{:S(2)}) copy-start(bf16[512,2048]{1,0:T(8,128)(2,1)} %copy-done.30) | copy-start | bytes 6291460
  494.9 23.2 %collective-permute-start.2 = (f32[8192]{0:T(1024)S(1)}, f32[8192]{0:T(1024)S(1)}, u32[]{:S(2)}, u32[]{:S(2)}) collective-permute-start(f32[8192]{0:T(1024)S(1)} %pad_maximum_fusion.9), channel_id=1, source_target_pairs={{0,1},{1,0},{2,3},{3,2},{4,5},{5,4},{6,7},{7,6},{8,9},{9,8},{10,11... | collective-permute-start | bytes 98312 | tf_op jit(solution)/shard_map/ppermute | solution.py:944
  496.5 4.4 copy-start.41
  496.5 4.4 copy-start.58
  668.8 7.3 %copy-start.4 = (f32[512,2048]{1,0:T(8,128)S(1)}, f32[512,2048]{1,0:T(8,128)}, u32[]{:S(2)}) copy-start(f32[512,2048]{1,0:T(8,128)} %get-tuple-element.117) | copy-start | bytes 12582916
  668.8 7.3 %copy-start.12 = (bf16[256,2048]{1,0:T(8,128)(2,1)S(1)}, bf16[256,2048]{1,0:T(8,128)(2,1)}, u32[]{:S(2)}) copy-start(bf16[256,2048]{1,0:T(8,128)(2,1)} %get-tuple-element.64) | copy-start | bytes 3145732
  672.6 3.5 copy-start.1
  672.6 4.2 copy-start.11
  672.6 4.2 slice-start
  678.9 3.6 copy-start.25
  (18 other events, 31.5 us)
Sparse Core Ops, SparseCore 0:
  99.2 94.4 all-gather.1
  389.9 126.2 reduce-scatter.1
where the time goes:
time: 696 us; the launch traced here: 691 us
  Pallas kernels  426 us (61%)
  matrix products  124 us (18%)
  local copies, waits for them, and re-layouts  57.2 us (8%)
  other arithmetic  42.7 us (6%)
  waiting for transfers between devices  21.3 us (3%)
  between operations  15.1 us (2%)
    pallas_call x2, Pallas kernels, ring_call(): pl.pallas_call(functools.partial(ring_kernel, chips, gathers, swaps, tupl...  234 us
    pallas_call x1, Pallas kernels, feed_call(): pl.pallas_call(functools.partial(feed_kernel, chips, tile), out_shape=[ja...  120 us
    pallas_call x1, Pallas kernels, back_call(): pl.pallas_call(functools.partial(back_kernel, chips, tile), out_shape=[ja...  72.3 us
    unnamed x128, local copies, waits for them, and re-layouts  24.1 us
    ppermute x3, waiting for transfers between devices, swap(): return lax.ppermute(values, 'mp', [(0, 1), (1, 0)])  21.3 us
    dot_general x3, matrix products, body(): jnp.dot(part, full.T, preferred_element_type=jnp.float32)  17.7 us
    dot_general x3, matrix products, body(): jnp.dot(normed_one, full, preferred_element_type=jnp.float32) + bias  17.7 us
    dot_general x3, matrix products, body(): jnp.dot(normed_one.T, part, preferred_element_type=jnp.float32)  14 us
  transfers between devices with their start and end apart: 5, of which 2 were waited for; matrix products, arithmetic and copies ran while one was open for 30% of the time, Pallas kernels for 21%

commit v1 on v0

--- a/solution.py
+++ b/solution.py
@@ -40,16 +40,19 @@
     )
 
 
-def ring_kernel(chips, gathers, swaps, groups, *refs):
+def ring_kernel(chips, bundles, swaps, groups, *refs):
     refs = list(refs)
-    scatters = sum(groups)
+    scatters, gathers = sum(groups), sum(bundles)
 
     def take(number):
         taken = refs[:number]
         del refs[:number]
         return taken
 
-    shards, sends, parts = take(gathers), take(swaps), take(scatters)
+    bundled, sends, parts = take(len(bundles)), take(swaps), take(scatters)
+    shards = []
+    for bundle, ref in zip(bundles, bundled):
+        shards += [ref] if bundle == 1 else [ref.at[j] for j in range(bundle)]
     fulls, gets, grouped = take(gathers), take(swaps), take(len(groups))
     outs = []
     for group, out in zip(groups, grouped):
@@ -203,8 +206,12 @@
 def ring_call(call_id, shards=(), sends=(), parts=(), groups=()):
     size = lax.axis_size("dp")
     chips = size // 2
-    gathers, swaps, scatters = len(shards), len(sends), len(parts)
-    outs = [jax.ShapeDtypeStruct((s.shape[0] * size, s.shape[1]), s.dtype) for s in shards]
+    bundles = [1 if s.ndim == 2 else s.shape[0] for s in shards]
+    gathers, swaps, scatters = sum(bundles), len(sends), len(parts)
+    outs = []
+    for bundle, s in zip(bundles, shards):
+        rows, cols = s.shape[-2:]
+        outs += [jax.ShapeDtypeStruct((rows * size, cols), s.dtype)] * bundle
     outs += [jax.ShapeDtypeStruct(s.shape, s.dtype) for s in sends]
     first = 0
     for group in groups:
@@ -226,9 +233,9 @@
     moved = sum(s.size * 2 * size for s in shards) + sum(p.size * 2 for p in parts)
     return list(
         pl.pallas_call(
-            functools.partial(ring_kernel, chips, gathers, swaps, tuple(groups)),
+            functools.partial(ring_kernel, chips, tuple(bundles), swaps, tuple(groups)),
             out_shape=outs,
-            in_specs=[pl.BlockSpec(memory_space=pltpu.VMEM)] * gathers
+            in_specs=[pl.BlockSpec(memory_space=pltpu.VMEM)] * len(shards)
             + [pl.BlockSpec(memory_space=pl.ANY)] * (swaps + scatters),
             out_specs=[pl.BlockSpec(memory_space=pl.ANY)] * len(outs),
             scratch_shapes=scratch,
@@ -978,7 +985,7 @@
     width = inputs.shape[1]
     *qkv_full, out_turned, far_inputs, far_cot = ring_call(
         0,
-        shards=[qkv_weight[0], qkv_weight[1], qkv_weight[2], out_weight.T],
+        shards=[qkv_weight, out_weight.T],
         sends=[inputs, cotangent],
     )
     input_rows = jnp.concatenate([inputs, far_inputs], axis=0)
@@ -1042,12 +1049,15 @@
     middle_rows = grow(middle_low)
     up_term = jnp.dot(normed_two.T, up_act, preferred_element_type=jnp.float32)
     feed_part = jnp.dot(hidden, down_turned.T, preferred_element_type=jnp.float32)
+    feed_low, middle_rows = lax.optimization_barrier(
+        (feed_part[rows_here:].astype(jnp.bfloat16), middle_rows)
+    )
+    feed_far = swap(feed_low)
+    feed = feed_part[:rows_here] + feed_far.astype(jnp.float32)
+    output = (middle + feed).astype(jnp.bfloat16)
     out_term = jnp.dot(middle_rows.T, mixed, preferred_element_type=jnp.float32)
-    mixed_grad = (
-        jnp.dot(middle_rows, out_turned, preferred_element_type=jnp.float32)
-        .astype(jnp.bfloat16)
-        .reshape(seq_len, head_count, HEAD_DIM)
-    )
+    mixed_flat = jnp.dot(middle_rows, out_turned, preferred_element_type=jnp.float32)
+    mixed_grad = mixed_flat.astype(jnp.bfloat16).reshape(seq_len, head_count, HEAD_DIM)
     probs_wide = jnp.exp(scores - log_total)
     value_grad = jnp.einsum(
         "hqk,qhd->khd",
@@ -1075,9 +1085,8 @@
     proj_low = [part.astype(jnp.bfloat16) for part in proj_grad]
     normed_one_part = jnp.zeros((), jnp.float32)
     for part, full in zip(proj_low, qkv_full):
-        normed_one_part = normed_one_part + jnp.dot(
-            part, full.T, preferred_element_type=jnp.float32
-        )
+        product = jnp.dot(part, full.T, preferred_element_type=jnp.float32)
+        normed_one_part = normed_one_part + product
     gain_one = jnp.sum(normed_one_part * scaled_rows, axis=0)
     shift_one = jnp.sum(normed_one_part, axis=0)
     norm_sums = jnp.concatenate([gain_one, shift_one, gain_two, shift_two])
@@ -1087,17 +1096,16 @@
     qkv_term = [
         jnp.dot(normed_one.T, part, preferred_element_type=jnp.float32) for part in proj_low
     ]
-    all_sums, far_part, far_feed, up_weight_grad, out_grad_turned, qkv_weight_grad = ring_call(
+    output, sums = lax.optimization_barrier((output, sums))
+    all_sums, far_part, up_weight_grad, out_grad_turned, qkv_weight_grad = ring_call(
         2,
         shards=[jnp.pad(sums, (0, spare)).reshape(8, -1)],
-        sends=[part[rows_here:].astype(jnp.bfloat16) for part in (normed_one_part, feed_part)],
+        sends=[normed_one_part[rows_here:].astype(jnp.bfloat16)],
         parts=[term.astype(jnp.bfloat16) for term in [up_term, out_term] + qkv_term],
         groups=[1, 1, 3],
     )
     out_weight_grad = out_grad_turned.T
     normed_one_grad = normed_one_part[:rows_here] + far_part.astype(jnp.float32)
-    feed = feed_part[:rows_here] + far_feed.astype(jnp.float32)
-    output = (middle + feed).astype(jnp.bfloat16)
     all_sums = jnp.sum(all_sums.reshape(-1, 8, all_sums.shape[1]), axis=0).reshape(-1)
     gain_one, shift_one, gain_two, shift_two = all_sums[: 4 * width].reshape(4, width)
     qkv_bias_grad = all_sums[4 * width : sums.size].reshape(3, local_width)

time: 696 us -> 697 us (level)
    ppermute x3 -> x4, waiting for transfers between devices: 21.3 us -> 23.8 us  [swap(): return lax.ppermute(values, 'mp', [(0, 1), (1, 0)])]
    unnamed x128 -> x129, local copies, waits for them, and re-layouts: 24.1 us -> 22.5 us
  transfers between devices with their start and end apart: 5 -> 6, of which waited for: 2 -> 3; matrix products, arithmetic and copies ran while one was open for 30% -> 30% of each run, Pallas kernels for 21% -> 21%
where the time goes in v1:
time: 697 us; the launch traced here: 692 us
  Pallas kernels  426 us (61%)
  matrix products  124 us (18%)
  local copies, waits for them, and re-layouts  52.3 us (8%)
  other arithmetic  45.9 us (7%)
  waiting for transfers between devices  23.8 us (3%)
  between operations  15.1 us (2%)
    pallas_call x2, Pallas kernels, ring_call(): pl.pallas_call(functools.partial(ring_kernel, chips, tuple(bundles), swap...  234 us
    pallas_call x1, Pallas kernels, feed_call(): pl.pallas_call(functools.partial(feed_kernel, chips, tile), out_shape=[ja...  120 us
    pallas_call x1, Pallas kernels, back_call(): pl.pallas_call(functools.partial(back_kernel, chips, tile), out_shape=[ja...  72.2 us
    ppermute x4, waiting for transfers between devices, swap(): return lax.ppermute(values, 'mp', [(0, 1), (1, 0)])  23.8 us
    unnamed x129, local copies, waits for them, and re-layouts  22.5 us
    dot_general x3, matrix products, body(): product = jnp.dot(part, full.T, preferred_element_type=jnp.float32)  17.8 us
    dot_general x3, matrix products, body(): jnp.dot(normed_one, full, preferred_element_type=jnp.float32) + bias  17.7 us
    dot_general x3, matrix products, body(): jnp.dot(normed_one.T, part, preferred_element_type=jnp.float32)  14.1 us
  transfers between devices with their start and end apart: 6, of which 3 were waited for; matrix products, arithmetic and copies ran while one was open for 30% of the time, Pallas kernels for 21%

profile of v1, /device:TPU:0, one launch (start us, length us, event | category | flops | bytes accessed | tf_op | source)
XLA Modules:
  0.0 692.2 jit_solution(13621579544914675917)
XLA Ops:
  7.2 1.9 copy.44
  9.1 87.9 %shard_map.220 = (bf16[2048,1024]{1,0:T(8,128)(2,1)}, bf16[2048,1024]{1,0:T(8,128)(2,1)}, bf16[2048,1024]{1,0:T(8,128)(2,1)}, bf16[2048,1024]{1,0:T(8,128)(2,1)}...) custom-call(bf16[3,128,1024]{2,1,0:T(8,128)(2,1)} %refs_0_.1, bf16[128,1024]{1,0:T(8,128)(2,1)} %bitcast.75, ...), custom_call_target="tpu_custom_call" | custom-call | bytes 16777216 | tf_op jit(solution)/shard_map/pallas_call | solution.py:235
  99.6 5.5 add_convert_fusion.2
  105.2 2.0 copy.45
  107.2 6.3 convolution_add_fusion
  113.5 2.9 copy.47
  116.4 2.4 slice.172
  118.8 5.9 convolution_add_fusion.1
  124.8 2.9 copy.46
  127.6 2.4 slice.173
  132.9 11.1 %fusion.32 = (f32[16,512]{1,0:T(8,128)S(1)}, f32[16,512,512]{1,2,0:T(8,128)}) fusion(bf16[512,16,48]{0,2,1:T(8,128)(2,1)} %slice.172, bf16[512,16,8]{0,2,1:T(8,128)(2,1)S(1)} %get-tuple-element.130, bf16[512,16,8]{0,2,1:T(8,128)(2,1)S(1)} %get-tuple-element.131, bf16[512,16,48]{0,2,1:T(8,128)(2,1)} %slice.173, ...), kind=kOutput, calls=%fused_computation.112 | convolution fusion | flops 555737088 | bytes 19169280 | tf_op jit(solution)/shard_map/qhd,khd->hqk/dot_general | solution.py:945
  144.0 8.4 %fusion = f32[16,512]{1,0:T(8,128)S(1)} fusion(f32[16,512,512]{1,2,0:T(8,128)} %get-tuple-element.139, f32[16,512]{1,0:T(8,128)S(1)} %get-tuple-element.138), kind=kLoop, calls=%fused_computation.5 | loop fusion | flops 8380416 | bytes 16842752 | tf_op jit(solution)/shard_map/reduce_sum | solution.py:1021
  152.4 8.0 %fusion.10 = bf16[16,64,512]{2,1,0:T(8,128)(2,1)S(1)} fusion(bf16[512,16,64]{0,2,1:T(8,128)(2,1)S(1)} %bitcast.68, f32[16,512,512]{1,2,0:T(8,128)} %get-tuple-element.139, f32[16,512]{1,0:T(8,128)S(1)} %fusion, f32[16,512]{1,0:T(8,128)S(1)} %get-tuple-element.138), kind=kOutput, calls=%fused_computation.55 | convolution fusion | flops 549978112 | bytes 18939904 | tf_op jit(solution)/shard_map/hqk,khd->qhd/dot_general | solution.py:1024
  160.5 2.4 fusion.33
  162.9 1.9 copy-done.18
  167.5 2.2 copy.49
  170.8 2.3 constant_dynamic-update-slice_fusion.cot_ref
  173.1 3.9 copy.50.cot_ref
  177.5 14.0 %collective-permute-done = bf16[256,2048]{1,0:T(8,128)(2,1)} collective-permute-done((bf16[256,2048]{1,0:T(8,128)(2,1)}, bf16[256,2048]{1,0:T(8,128)(2,1)}, u32[]{:S(2)}, u32[]{:S(2)}) %collective-permute-start) | collective-permute-done | bytes 1048608 | tf_op jit(solution)/shard_map/ppermute | solution.py:951
  195.7 119.7 %shard_map.221 = (bf16[2048,2816]{1,0:T(8,128)(2,1)}, bf16[2048,2816]{1,0:T(8,128)(2,1)}, bf16[512,2048]{1,0:T(8,128)(2,1)}, f32[512,2816]{1,0:T(8,128)}, f32[51...) custom-call(bf16[128,2816]{1,0:T(8,128)(2,1)} %up_shard.1, bf16[128,2816]{1,0:T(8,128)(2,1)} %bitcast.78, ...), custom_call_target="tpu_custom_call" | custom-call | flops 17716740096 | bytes 86507520 | tf_op jit(solution)/shard_map/pallas_call | solution.py:497
  315.4 72.2 %shard_map.222 = (bf16[512,2816]{1,0:T(8,128)(2,1)}, bf16[512,2816]{1,0:T(8,128)(2,1)}, f32[256,2048]{1,0:T(8,128)}, bf16[256,2048]{1,0:T(8,128)(2,1)}, f32[128,2816]{1,0:T(8,128)}, /*index=5*/bf16[2048,2816]{1,0:T(8,128)(2,1)}) custom-call(bf16[512,2048]{1,0:T(8,128)(2,1)} %constant_dynamic-update-slice_fusion.cot_ref, ...), custom_call_target="tpu_custom_call" | custom-call | flops 23622320128 | bytes 63438848 | tf_op jit(solution)/shard_map/pallas_call | solution.py:858
  389.3 3.5 multiply_reduce_fusion.3
  392.9 2.7 fusion.27
  395.6 9.8 %fusion.34 = f32[512,2048]{1,0:T(8,128)S(1)} fusion(bf16[512,2816]{1,0:T(8,128)(2,1)S(1)} %copy-done.60, bf16[2048,2816]{1,0:T(8,128)(2,1)} %get-tuple-element.57.down_full), kind=kOutput, calls=%fused_computation.114 | convolution fusion | flops 5905580032 | bytes 18612224 | tf_op jit(solution)/shard_map/dot_general | solution.py:1051
  405.4 2.0 copy-done.17
  409.7 3.0 copy.57
  412.6 11.0 %convolution_convert_fusion.refs_2_ = bf16[2048,2816]{1,0:T(8,128)(2,1)} fusion(bf16[512,2048]{1,0:T(8,128)(2,1)} %get-tuple-element.53.normed_ref, bf16[512,2816]{1,0:T(8,128)(2,1)} %get-tuple-element.69), kind=kOutput, calls=%fused_computation.7 | convolution fusion | flops 5911347200 | bytes 16515072 | tf_op jit(solution)/shard_map/dot_general | solution.py:1050
  423.7 8.7 %collective-permute-done.1 = bf16[256,2048]{1,0:T(8,128)(2,1)} collective-permute-done((bf16[256,2048]{1,0:T(8,128)(2,1)}, bf16[256,2048]{1,0:T(8,128)(2,1)}, u32[]{:S(2)}, u32[]{:S(2)}) %collective-permute-start.1) | collective-permute-done | bytes 1048608 | tf_op jit(solution)/shard_map/ppermute | solution.py:951
  435.6 3.3 convolution_convert_fusion.5
  438.9 2.3 copy.51
  441.2 1.9 multiply_reduce_fusion.4
  443.1 11.2 %multiply_convert_fusion = bf16[16,512,512]{1,2,0:T(8,128)(2,1)S(1)} fusion(f32[16,512,512]{1,2,0:T(8,128)} %get-tuple-element.139, bf16[512,16,64]{0,2,1:T(8,128)(2,1)} %bitcast.60, bf16[512,16,64]{0,2,1:T(8,128)(2,1)} %bitcast.69, f32[16,512]{1,0:T(8,128)S(1)} %bitcast.80, f32[16,512]{1,0:T(8,128)} %log_add_fusion), kind=kOutput, calls=%fused_computation | convolution fusion | flops 557842432 | bytes 27328512 | tf_op jit(solution)/shard_map/qhd,khd->hqk/dot_general | solution.py:1068
  454.3 2.6 convolution_bitcast_fusion
  466.8 4.5 fusion.35
  471.4 4.3 fusion.36
  475.7 9.0 %bitcast_reduce_fusion = (f32[16,64]{1,0:T(8,128)S(1)}, bf16[16,64,512]{2,1,0:T(8,128)(2,1)S(1)}) fusion(bf16[512,16,64]{0,2,1:T(8,128)(2,1)S(1)} %bitcast.61, f32[16,512,512]{1,2,0:T(8,128)} %get-tuple-element.139, f32[16,512]{1,0:T(8,128)S(1)} %copy-done.33), kind=kOutput, calls=%fused_computation.35 | convolution fusion | flops 546307072 | bytes 18911232 | tf_op jit(solution)/shard_map/hqk,qhd->khd/dot_general | solution.py:1062
  484.8 9.0 %multiply_reduce_fusion = (f32[2048]{0:T(1024)S(1)}, f32[2048]{0:T(1024)S(1)}, f32[512,2048]{1,0:T(8,128)}, f32[512,2048]{1,0:T(8,128)}) fusion(f32[512]{0:T(512)S(1)} %copy-done.50, f32[512]{0:T(512)S(1)} %copy-done.46, bf16[256,2048]{1,0:T(8,128)(2,1)S(1)} %copy-done.3, bf16[256,2048]{1,0:T(8,128)(2,1)S(1)} %copy-done, ...), kind=kOutput, calls=%fused_computation.11 | convolution fusion | flops 2159013888 | bytes 24137728 | tf_op jit(solution)/shard_map/dot_general | solution.py:1088
  496.0 4.4 convolution_convert_fusion.4.refs_3_
  500.4 4.6 convolution_convert_fusion.1.refs_6_
  505.0 4.7 convolution_convert_fusion.2.refs_5_
  509.7 4.7 convolution_convert_fusion.3.refs_4_
  514.8 2.7 slice.169.refs_1_
  518.6 3.3 fusion.8
  522.5 146.3 %shard_map.223 = (f32[128,1536]{1,0:T(8,128)}, bf16[256,2048]{1,0:T(8,128)(2,1)}, f32[128,2816]{1,0:T(8,128)}, f32[128,1024]{1,0:T(8,128)}, f32[3,128,1024]{2,1,0:T(8,128)}) custom-call(f32[8,1536]{1,0:T(8,128)} %reshape.269.refs_0_, bf16[256,2048]{1,0:T(8,128)(2,1)} %slice.169.refs_1_, bf16[2048,2816]{1,0:T(8,128)(2,1)} %convolution_convert_fusion.refs_2_, ...), custom_call_target="tpu_custom_call" | custom-call | bytes 28704768 | tf_op jit(solution)/shard_map/pallas_call | solution.py:235
  670.7 2.2 copy.56
  672.9 3.2 fusion.15
  676.8 3.6 multiply_add_fusion
  680.4 2.5 convert_element_type.142
  (187 shorter events, 39.5 us)
Async XLA Ops:
  7.2 90.0 %copy-start = (bf16[256,2048]{1,0:T(8,128)(2,1)S(1)}, bf16[256,2048]{1,0:T(8,128)(2,1)}, u32[]{:S(2)}) copy-start(bf16[256,2048]{1,0:T(8,128)(2,1)} %refs_2_.1) | copy-start | bytes 3145732
  7.2 188.5 %all-gather.2.cloned.1.call-start = ((), (), s32[]{:S(2)}) async-start(), calls=%async_computation.1 | async-start | bytes 12255232 | tf_op jit(solution)/shard_map/all_gather | solution.py:994
  97.1 583.3 %reduce-scatter.2.cloned.1.call-start = ((), (), s32[]{:S(2)}) async-start(), calls=%async_computation.2 | async-start | bytes 12255232 | tf_op jit(solution)/shard_map/reduce_scatter | solution.py:965
  98.9 20.0 %copy-start.45 = (f32[512]{0:T(512)}, f32[512]{0:T(512)S(1)}, u32[]{:S(2)}) copy-start(f32[512]{0:T(512)S(1)} %broadcast_multiply_fusion.1) | copy-start | bytes 6148
  99.6 19.2 %copy-start.49 = (f32[512]{0:T(512)}, f32[512]{0:T(512)S(1)}, u32[]{:S(2)}) copy-start(f32[512]{0:T(512)S(1)} %add_rsqrt_fusion) | copy-start | bytes 6148
  107.2 45.2 %copy-start.14 = (bf16[512,1024]{0,1:T(8,128)(2,1)}, bf16[512,1024]{0,1:T(8,128)(2,1)S(1)}, u32[]{:S(2)}) copy-start(bf16[512,1024]{0,1:T(8,128)(2,1)S(1)} %copy.45) | copy-start | bytes 3145732
  124.7 5.3 copy-start.53
  132.8 11.1 %copy-start.31 = (bf16[512,16,8]{0,2,1:T(8,128)(2,1)}, bf16[512,16,8]{0,2,1:T(8,128)(2,1)S(1)}, u32[]{:S(2)}) copy-start(bf16[512,16,8]{0,2,1:T(8,128)(2,1)S(1)} %get-tuple-element.120) | copy-start | bytes 393220
  144.0 8.4 %copy-start.34 = (f32[16,512]{1,0:T(8,128)}, f32[16,512]{1,0:T(8,128)S(1)}, u32[]{:S(2)}) copy-start(f32[16,512]{1,0:T(8,128)S(1)} %get-tuple-element.138) | copy-start | bytes 98308
  152.4 8.1 %copy-start.35 = (f32[16,512]{1,0:T(8,128)}, f32[16,512]{1,0:T(8,128)S(1)}, u32[]{:S(2)}) copy-start(f32[16,512]{1,0:T(8,128)S(1)} %fusion) | copy-start | bytes 98308
  152.4 8.0 %copy-start.56 = (bf16[2048,1024]{1,0:T(8,128)(2,1)S(1)}, bf16[2048,1024]{1,0:T(8,128)(2,1)}, u32[]{:S(2)}) copy-start(bf16[2048,1024]{1,0:T(8,128)(2,1)} %get-tuple-element.50) | copy-start | bytes 12582916
  164.8 4.9 copy-start.7
  165.9 25.6 %collective-permute-start = (bf16[256,2048]{1,0:T(8,128)(2,1)}, bf16[256,2048]{1,0:T(8,128)(2,1)}, u32[]{:S(2)}, u32[]{:S(2)}) collective-permute-start(bf16[256,2048]{1,0:T(8,128)(2,1)} %slice.171), channel_id=1, source_target_pairs={{0,1},{1,0},{2,3},{3,2},{4,5},{5,4},{6,7},{7,6},{8,9},{9,8},{10,11... | collective-permute-start | bytes 3145736 | tf_op jit(solution)/shard_map/ppermute | solution.py:951
  177.0 14.6 %copy-start.19 = (f32[512,2048]{1,0:T(8,128)S(1)}, f32[512,2048]{1,0:T(8,128)}, u32[]{:S(2)}) copy-start(f32[512,2048]{1,0:T(8,128)} %copy-done.18) | copy-start | bytes 12582916
  177.5 16.8 %copy-start.36 = (f32[2048]{0:T(1024)S(1)}, f32[2048]{0:T(1024)}, u32[]{:S(2)}) copy-start(f32[2048]{0:T(1024)} %param.22) | copy-start | bytes 24580
  177.5 16.8 %copy-start.52 = (f32[2048]{0:T(1024)S(1)}, f32[2048]{0:T(1024)}, u32[]{:S(2)}) copy-start(f32[2048]{0:T(1024)} %param.23) | copy-start | bytes 24580
  387.7 5.2 copy-start.8
  387.7 5.2 copy-start.9
  387.7 5.2 copy-start.12
  387.7 5.2 copy-start.37
  387.8 5.2 copy-start.44
  387.8 5.2 copy-start.48
  408.5 23.9 %collective-permute-start.1 = (bf16[256,2048]{1,0:T(8,128)(2,1)}, bf16[256,2048]{1,0:T(8,128)(2,1)}, u32[]{:S(2)}, u32[]{:S(2)}) collective-permute-start(bf16[256,2048]{1,0:T(8,128)(2,1)} %get-tuple-element.64), channel_id=1, source_target_pairs={{0,1},{1,0},{2,3},{3,2},{4,5},{5,4},{6,7},{7,6},{8,9},{9,8},{10,11... | collective-permute-start | bytes 3145736 | tf_op jit(solution)/shard_map/ppermute | solution.py:951
  423.7 11.9 %copy-start.57 = (bf16[2048,1024]{1,0:T(8,128)(2,1)S(1)}, bf16[2048,1024]{1,0:T(8,128)(2,1)}, u32[]{:S(2)}) copy-start(bf16[2048,1024]{1,0:T(8,128)(2,1)} %get-tuple-element.50) | copy-start | bytes 12582916
  443.1 11.2 %copy-start.16 = (bf16[512,16,48]{0,2,1:T(8,128)(2,1)S(1)}, bf16[512,16,48]{0,2,1:T(8,128)(2,1)}, u32[]{:S(2)}) copy-start(bf16[512,16,48]{0,2,1:T(8,128)(2,1)} %slice.173) | copy-start | bytes 2359300
  443.1 11.2 %copy-start.32 = (bf16[512,16,8]{0,2,1:T(8,128)(2,1)S(1)}, bf16[512,16,8]{0,2,1:T(8,128)(2,1)}, u32[]{:S(2)}) copy-start(bf16[512,16,8]{0,2,1:T(8,128)(2,1)} %copy-done.31) | copy-start | bytes 393220
  462.9 3.9 copy-start.55
  465.2 6.2 copy-start.27
  466.8 4.5 copy-start.54
  471.4 4.3 copy-start.4
  471.4 4.3 copy-start.33
  475.7 9.1 %copy-start.3 = (bf16[256,2048]{1,0:T(8,128)(2,1)S(1)}, bf16[256,2048]{1,0:T(8,128)(2,1)}, u32[]{:S(2)}) copy-start(bf16[256,2048]{1,0:T(8,128)(2,1)} %get-tuple-element.45) | copy-start | bytes 3145732
  475.7 9.1 %copy-start.13 = (bf16[2048,1024]{1,0:T(8,128)(2,1)S(1)}, bf16[2048,1024]{1,0:T(8,128)(2,1)}, u32[]{:S(2)}) copy-start(bf16[2048,1024]{1,0:T(8,128)(2,1)} %get-tuple-element.46) | copy-start | bytes 12582916
  475.7 9.1 %copy-start.46 = (f32[512]{0:T(512)S(1)}, f32[512]{0:T(512)}, u32[]{:S(2)}) copy-start(f32[512]{0:T(512)} %copy-done.45) | copy-start | bytes 6148
  475.7 9.1 %copy-start.50 = (f32[512]{0:T(512)S(1)}, f32[512]{0:T(512)}, u32[]{:S(2)}) copy-start(f32[512]{0:T(512)} %copy-done.49) | copy-start | bytes 6148
  484.8 9.0 %copy-start.38 = (f32[2048]{0:T(1024)S(1)}, f32[2048]{0:T(1024)}, u32[]{:S(2)}) copy-start(f32[2048]{0:T(1024)} %get-tuple-element.103) | copy-start | bytes 24580
  484.8 9.0 %copy-start.39 = (f32[2048]{0:T(1024)S(1)}, f32[2048]{0:T(1024)}, u32[]{:S(2)}) copy-start(f32[2048]{0:T(1024)} %get-tuple-element.108) | copy-start | bytes 24580
  484.8 11.1 %copy-start.24 = (bf16[512,2048]{1,0:T(8,128)(2,1)S(1)}, bf16[512,2048]{1,0:T(8,128)(2,1)}, u32[]{:S(2)}) copy-start(bf16[512,2048]{1,0:T(8,128)(2,1)} %copy-done.23) | copy-start | bytes 6291460
  484.8 11.1 %copy-start.30 = (bf16[16,64,512]{2,1,0:T(8,128)(2,1)S(1)}, bf16[16,64,512]{2,1,0:T(8,128)(2,1)}, u32[]{:S(2)}) copy-start(bf16[16,64,512]{2,1,0:T(8,128)(2,1)} %copy-done.29) | copy-start | bytes 3145732
  493.9 23.7 %collective-permute-start.3 = (f32[8192]{0:T(1024)S(1)}, f32[8192]{0:T(1024)S(1)}, u32[]{:S(2)}, u32[]{:S(2)}) collective-permute-start(f32[8192]{0:T(1024)S(1)} %pad_maximum_fusion.11), channel_id=1, source_target_pairs={{0,1},{1,0},{2,3},{3,2},{4,5},{5,4},{6,7},{7,6},{8,9},{9,8},{10,11... | collective-permute-start | bytes 98312 | tf_op jit(solution)/shard_map/ppermute | solution.py:951
  495.4 23.2 %collective-permute-start.2 = (bf16[256,2048]{1,0:T(8,128)(2,1)}, bf16[256,2048]{1,0:T(8,128)(2,1)}, u32[]{:S(2)}, u32[]{:S(2)}) collective-permute-start(bf16[256,2048]{1,0:T(8,128)(2,1)} %slice.170), channel_id=1, source_target_pairs={{0,1},{1,0},{2,3},{3,2},{4,5},{5,4},{6,7},{7,6},{8,9},{9,8},{10,11... | collective-permute-start | bytes 3145736 | tf_op jit(solution)/shard_map/ppermute | solution.py:951
  496.0 4.4 copy-start.42
  496.0 4.4 copy-start.59
  505.0 4.7 copy-start.28
  668.8 8.0 %copy-start.11 = (bf16[256,2048]{1,0:T(8,128)(2,1)S(1)}, bf16[256,2048]{1,0:T(8,128)(2,1)}, u32[]{:S(2)}) copy-start(bf16[256,2048]{1,0:T(8,128)(2,1)} %get-tuple-element.70) | copy-start | bytes 3145732
  670.7 6.0 copy-start.10
  672.9 3.9 copy-start.1
  672.9 3.9 slice-start
  (20 other events, 38.9 us)
Sparse Core Ops, SparseCore 0:
  97.2 94.4 all-gather.1
  387.8 126.2 reduce-scatter.1
